TPU v7x, 32 devices: a whole 2x2x4 slice. The times are simulated.
32 devices in a mesh: shard: 8 (over y, x, core), width: 4 (over z).
Axes of the slice: x: 2, y: 2, z: 4, core: 2. Of those that a mesh axis runs over, the one named last changes fastest.
Arguments:
- w_query: bfloat16 [5120, 5120], P('shard', 'width'), may hold values from -0.125 to 0.125
- low_query: bfloat16 [5120, 32], P('shard'), may hold values from -0.078125 to 0.078125
- high_query: bfloat16 [32, 5120], P(None, 'width'), may hold values from -1 to 1
- w_key: bfloat16 [5120, 5120], P('shard', 'width'), may hold values from -0.125 to 0.125
- low_key: bfloat16 [5120, 32], P('shard'), may hold values from -0.078125 to 0.078125
- high_key: bfloat16 [32, 5120], P(None, 'width'), may hold values from -1 to 1
- w_value: bfloat16 [5120, 5120], P('shard', 'width'), may hold values from -0.125 to 0.125
- low_value: bfloat16 [5120, 32], P('shard'), may hold values from -0.078125 to 0.078125
- high_value: bfloat16 [32, 5120], P(None, 'width'), may hold values from -1 to 1
- norm_train: float32 [5120], P(('shard', 'width')), may hold values from 0.25 to 1.75
- norm_step: float32 [5120], P(('shard', 'width')), may hold values from -0.3 to 0.3
Outputs:
- ready_query: bfloat16 [5120, 5120], P(None, 'width')
- ready_key: bfloat16 [5120, 5120], P(None, 'width')
- ready_value: bfloat16 [5120, 5120], P(None, 'width')
- factor_query: float32 [5120], P('width')
- factor_key: float32 [5120], P('width')
- factor_value: float32 [5120], P('width')
- serve_norm: bfloat16 [5120], replicated
All inputs are finite; a program needn't handle non-finite values. Where the computation divides by a largest or mean magnitude, that divisor is 1e-20 or more.
Results may differ from a plain program's by a relative error of at most 0.001.
Values may be sent and summed in bfloat16 or wider, within the bound.
A program may use at most 128 MiB of HBM per device.

v0:
```python
import jax
import jax.numpy as jnp
from jax import lax
from jax.sharding import PartitionSpec as P

mix_rate = 0.5


def body(
    w_query,
    low_query,
    high_query,
    w_key,
    low_key,
    high_key,
    w_value,
    low_value,
    high_value,
    norm_train,
    norm_step,
):
    latest_query = w_query.astype(jnp.float32) + mix_rate * jnp.dot(
        low_query, high_query, preferred_element_type=jnp.float32
    )
    latest_key = w_key.astype(jnp.float32) + mix_rate * jnp.dot(
        low_key, high_key, preferred_element_type=jnp.float32
    )
    latest_value = w_value.astype(jnp.float32) + mix_rate * jnp.dot(
        low_value, high_value, preferred_element_type=jnp.float32
    )
    factor_query, factor_key, factor_value = lax.pmax(
        (
            jnp.max(jnp.abs(latest_query), axis=0),
            jnp.max(jnp.abs(latest_key), axis=0),
            jnp.max(jnp.abs(latest_value), axis=0),
        ),
        "shard",
    )
    narrow_query, narrow_key, narrow_value = (
        (latest_query / factor_query).astype(jnp.bfloat16),
        (latest_key / factor_key).astype(jnp.bfloat16),
        (latest_value / factor_value).astype(jnp.bfloat16),
    )
    ready_query, ready_key, ready_value = (
        lax.all_gather(narrow_query, "shard", axis=0, tiled=True),
        lax.all_gather(narrow_key, "shard", axis=0, tiled=True),
        lax.all_gather(narrow_value, "shard", axis=0, tiled=True),
    )
    serve_norm = lax.all_gather(
        (norm_train + norm_step).astype(jnp.bfloat16), ("shard", "width"), axis=0, tiled=True
    )
    return (ready_query, ready_key, ready_value, factor_query, factor_key, factor_value, serve_norm)


def solution(mesh):
    return jax.shard_map(
        body,
        mesh=mesh,
        in_specs=(
            P("shard", "width"),
            P("shard", None),
            P(None, "width"),
            P("shard", "width"),
            P("shard", None),
            P(None, "width"),
            P("shard", "width"),
            P("shard", None),
            P(None, "width"),
            P(("shard", "width")),
            P(("shard", "width")),
        ),
        out_specs=(
            P(None, "width"),
            P(None, "width"),
            P(None, "width"),
            P("width"),
            P("width"),
            P("width"),
            P(),
        ),
        check_vma=False,
    )
```

profile of v0, /device:TPU:0, one launch (start us, length us, event | category | flops | bytes accessed | tf_op | source)
XLA Modules:
  0.0 304.8 jit_solution(4753450448453301033)
XLA Ops:
  7.2 0.0 copy-start
  7.2 0.0 all-gather.6.cloned.1.call-start
  7.3 0.8 copy-done
  8.1 2.2 abs_reduce_fusion.2
  10.3 0.0 copy-start.4
  10.3 0.0 copy-start.6
  10.3 0.0 copy-start.8
  10.3 2.3 abs_reduce_fusion.1
  12.7 2.3 abs_reduce_fusion
  15.0 25.5 %all-reduce.1 = (f32[1280]{0:T(1024)S(1)}, f32[1280]{0:T(1024)S(1)}, f32[1280]{0:T(1024)S(1)}) all-reduce(f32[1280]{0:T(1024)S(1)} %get-tuple-element.10, f32[1280]{0:T(1024)S(1)} %get-tuple-element.12, f32[1280]{0:T(1024)S(1)} %get-tuple-element.14), channel_id=1, replica_groups=mesh['shard'=8,'width'=4] {'shard'}, use_global_device_ids=true, to_apply=%region_1.0 | all-reduce | flops 3840 | bytes 30720 | tf_op jit(solution)/shard_map/pmax | solution.py:31
  40.6 0.0 copy-start.9
  40.6 3.3 %divide_convert_fusion.1 = bf16[640,1280]{1,0:T(8,128)(2,1)} fusion(f32[640,1280]{1,0:T(8,128)} %get-tuple-element.13, f32[1280]{0:T(1024)S(1)} %get-tuple-element.27), kind=kLoop, calls=%fused_computation.8 | loop fusion | flops 1638400 | bytes 4920320 | tf_op jit(solution)/shard_map/convert_element_type | solution.py:41
  43.9 0.0 all-gather.6.cloned.1.call-update
  43.9 0.0 all-gather.8.cloned.1.call-start
  44.0 3.3 %divide_convert_fusion = bf16[640,1280]{1,0:T(8,128)(2,1)} fusion(f32[640,1280]{1,0:T(8,128)} %get-tuple-element.15, f32[1280]{0:T(1024)S(1)} %get-tuple-element.28), kind=kLoop, calls=%fused_computation.6 | loop fusion | flops 1638400 | bytes 4920320 | tf_op jit(solution)/shard_map/convert_element_type | solution.py:42
  47.3 0.0 all-gather.8.cloned.1.call-update
  47.4 0.0 all-gather.4.cloned.1.call-start
  47.4 0.0 copy-start.12
  47.4 1.4 divide_convert_fusion.2
  48.8 0.0 all-gather.4.cloned.1.call-update
  48.9 0.2 dynamic-update-slice
  49.2 40.9 %all-reduce = bf16[5120]{0:T(1024)(128)(2,1)} all-reduce(bf16[5120]{0:T(1024)(128)(2,1)S(1)} %dynamic-update-slice), channel_id=1, replica_groups=mesh['shard'=8,'width'=4] {'shard','width'}, use_global_device_ids=true, to_apply=%add | all-reduce | flops 5120 | bytes 20480
  90.0 28.6 %all-gather.6.cloned.1.call-done = bf16[5120,1280]{1,0:T(8,128)(2,1)} async-done(((bf16[640,1280]{1,0:T(8,128)(2,1)}), bf16[5120,1280]{1,0:T(8,128)(2,1)}) %all-gather.6.cloned.1.call-update) | async-done | bytes 13107216 | tf_op jit(solution)/shard_map/all_gather | solution.py:46
  118.6 76.1 %all-gather.8.cloned.1.call-done = bf16[5120,1280]{1,0:T(8,128)(2,1)} async-done(((bf16[640,1280]{1,0:T(8,128)(2,1)}), bf16[5120,1280]{1,0:T(8,128)(2,1)}) %all-gather.8.cloned.1.call-update) | async-done | bytes 13107216 | tf_op jit(solution)/shard_map/all_gather | solution.py:47
  194.8 76.7 %all-gather.4.cloned.1.call-done = bf16[5120,1280]{1,0:T(8,128)(2,1)} async-done(((bf16[640,1280]{1,0:T(8,128)(2,1)}), bf16[5120,1280]{1,0:T(8,128)(2,1)}) %all-gather.4.cloned.1.call-update) | async-done | bytes 13107216 | tf_op jit(solution)/shard_map/all_gather | solution.py:45
  271.5 12.6 %copy.22 = bf16[5120,1280]{1,0:T(8,128)(2,1)} copy(bf16[5120,1280]{1,0:T(8,128)(2,1)} %all-gather.4.cloned.1.call-done) | data formatting | bytes 26214400
  284.1 0.1 copy-done.2
  284.3 6.6 %copy.23 = bf16[5120,1280]{1,0:T(8,128)(2,1)} copy(bf16[5120,1280]{1,0:T(8,128)(2,1)S(1)} %copy-done.2) | data formatting | bytes 26214400
  290.9 1.1 slice-done.1
  292.0 1.3 slice-done.2
  293.3 0.0 slice-done.3
  293.3 4.9 %copy.24 = bf16[5120,1280]{1,0:T(8,128)(2,1)} copy(bf16[5120,1280]{1,0:T(8,128)(2,1)S(1)} %bitcast.7) | data formatting | bytes 26214400
  (28 shorter events, 0.1 us)
Async XLA Ops:
  7.2 0.9 copy-start
  7.2 3.1 %copy-start.7 = (bf16[640,32]{0,1:T(8,128)(2,1)S(1)}, bf16[640,32]{0,1:T(8,128)(2,1)}, u32[]{:S(2)}) copy-start(bf16[640,32]{0,1:T(8,128)(2,1)} %param.15) | copy-start | bytes 122884
  7.2 3.1 %copy-start.5 = (bf16[32,1280]{1,0:T(8,128)(2,1)S(1)}, bf16[32,1280]{1,0:T(8,128)(2,1)}, u32[]{:S(2)}) copy-start(bf16[32,1280]{1,0:T(8,128)(2,1)} %param.16) | copy-start | bytes 245764
  7.2 111.4 %all-gather.6.cloned.1.call-start = ((), (), s32[]{:S(2)}) async-start(), calls=%async_computation.1 | async-start | bytes 14745600 | tf_op jit(solution)/shard_map/all_gather | solution.py:46
  8.1 2.2 copy-start.3
  10.3 2.4 copy-start.4
  10.3 2.4 copy-start.6
  10.3 2.4 copy-start.8
  40.6 3.4 %copy-start.10 = (f32[1280]{0:T(1024)}, f32[1280]{0:T(1024)S(1)}, u32[]{:S(2)}) copy-start(f32[1280]{0:T(1024)S(1)} %get-tuple-element.27) | copy-start | bytes 15364
  40.6 3.4 %copy-start.11 = (f32[1280]{0:T(1024)}, f32[1280]{0:T(1024)S(1)}, u32[]{:S(2)}) copy-start(f32[1280]{0:T(1024)S(1)} %get-tuple-element.28) | copy-start | bytes 15364
  40.6 6.8 %copy-start.9 = (f32[1280]{0:T(1024)}, f32[1280]{0:T(1024)S(1)}, u32[]{:S(2)}) copy-start(f32[1280]{0:T(1024)S(1)} %get-tuple-element.26) | copy-start | bytes 15364
  43.9 150.8 %all-gather.8.cloned.1.call-start = ((), (), s32[]{:S(2)}) async-start(), calls=%async_computation.2 | async-start | bytes 14745600 | tf_op jit(solution)/shard_map/all_gather | solution.py:47
  47.4 224.1 %all-gather.4.cloned.1.call-start = ((), (), s32[]{:S(2)}) async-start(), calls=%async_computation | async-start | bytes 14745600 | tf_op jit(solution)/shard_map/all_gather | solution.py:45
  47.4 1.5 copy-start.12
  47.4 1.5 copy-start.13
  271.5 12.8 %copy-start.2 = (bf16[5120,1280]{1,0:T(8,128)(2,1)S(1)}, bf16[5120,1280]{1,0:T(8,128)(2,1)}, u32[]{:S(2)}) copy-start(bf16[5120,1280]{1,0:T(8,128)(2,1)} %all-gather.6.cloned.1.call-done) | copy-start | bytes 39321604
  271.5 19.4 %slice-start = ((s8[13107200]{0:T(1024)(128)(4,1)}), s8[4194304]{0:T(1024)(128)(4,1)S(1)}, s32[]{:S(2)}) async-start(s8[13107200]{0:T(1024)(128)(4,1)} %bitcast.6), calls=%async_computation.3 | async-start | bytes 8388608
  271.5 20.5 %slice-start.1 = ((s8[13107200]{0:T(1024)(128)(4,1)}), s8[4194304]{0:T(1024)(128)(4,1)S(1)}, s32[]{:S(2)}) async-start(s8[13107200]{0:T(1024)(128)(4,1)} %bitcast.6), calls=%async_computation.4 | async-start | bytes 8388608
  284.3 9.0 %slice-start.2 = ((s8[13107200]{0:T(1024)(128)(4,1)}), s8[4194304]{0:T(1024)(128)(4,1)S(1)}, s32[]{:S(2)}) async-start(s8[13107200]{0:T(1024)(128)(4,1)} %bitcast.6), calls=%async_computation.5 | async-start | bytes 8388608
  284.3 9.0 %slice-start.3 = ((s8[13107200]{0:T(1024)(128)(4,1)}), s8[524288]{0:T(1024)(128)(4,1)S(1)}, s32[]{:S(2)}) async-start(s8[13107200]{0:T(1024)(128)(4,1)} %bitcast.6), calls=%async_computation.6 | async-start | bytes 1048576
  293.3 5.0 %copy-start.1 = (bf16[32,1280]{1,0:T(8,128)(2,1)S(1)}, bf16[32,1280]{1,0:T(8,128)(2,1)}, u32[]{:S(2)}) copy-start(bf16[32,1280]{1,0:T(8,128)(2,1)} %param.13) | copy-start | bytes 245764
Sparse Core Ops, SparseCore 0:
  44.1 74.5 all-gather.5
  120.5 74.1 all-gather.7
  197.2 74.1 all-gather.3
where the time goes:
time: 305 us
  waiting for transfers between devices  181 us (59%)
  blocking collectives  66.4 us (22%)
  local copies, waits for them, and re-layouts  27.9 us (9%)
  between operations  13.9 us (5%)
  other arithmetic  8.07 us (3%)
  matrix products  6.87 us (2%)
    all_gather x1, waiting for transfers between devices, body(): lax.all_gather(narrow_query, 'shard', axis=0, tiled=True)  76.7 us
    all_gather x1, waiting for transfers between devices, body(): lax.all_gather(narrow_value, 'shard', axis=0, tiled=True)  76.1 us
    unnamed x1, blocking collectives  40.9 us
    all_gather x1, waiting for transfers between devices, body(): lax.all_gather(narrow_key, 'shard', axis=0, tiled=True)  28.6 us
    unnamed x41, local copies, waits for them, and re-layouts  27.9 us
    pmax x1, blocking collectives, body(): lax.pmax((jnp.max(jnp.abs(latest_query), axis=0), jnp.max(jnp.abs(latest_...  25.5 us
  transfers between devices with their start and end apart: 3, of which 3 were waited for; matrix products, arithmetic and copies ran while one was open for 2% of the time, Pallas kernels for 0%

commit v1 on v0

v1 whole, which is shorter than its diff:
```python
import functools

import jax
import jax.numpy as jnp
from jax import lax
from jax.experimental import pallas as pl
from jax.experimental.pallas import tpu as pltpu
from jax.sharding import PartitionSpec as P

mix_rate = 0.5
MESH = pl.DeviceIdType.MESH
ANY = pl.BlockSpec(memory_space=pl.ANY)


def chunks_of(rows):
    for count in (5, 4, 2):
        if rows % (2 * count * 16) == 0:
            return count
    return 1


def gather_kernel(n, width, *refs):
    weights, lows, highs, norms = refs[0:3], refs[3:6], refs[6:9], refs[9:11]
    ready, factors, gains = refs[11], refs[12:15], refs[15]
    w_mem, low_mem, high_mem, norm_mem, latest, scale, maxima = refs[16:23]
    load_sem, send_sem, max_send, max_recv, norm_send, norm_recv = refs[23:29]
    ring_sem, pair_sem, low_turned = refs[29:32]
    outs = [ready.at[m] for m in range(3)]

    rows = w_mem.shape[1]
    chips = n // 2
    half = chips // 2
    count = chunks_of(rows)
    piece = rows // (2 * count)
    steps = 3 * count

    me = lax.axis_index("shard")
    line = lax.axis_index("width")
    chip, core = me // 2, lax.rem(me, 2)
    sibling = me + 1 - 2 * core

    def turned(c):
        return jnp.where(c < half, c, chips + half - 1 - c)

    place = turned(chip)

    def shard_at(offset):
        return turned(lax.rem(place + offset + 2 * chips, chips)) * 2 + core

    loads = []
    for m in range(3):
        group = []
        for source, target in (
            (weights[m], w_mem.at[m]),
            (lows[m], low_turned.at[m]),
            (highs[m], high_mem.at[m]),
        ):
            group.append(pltpu.make_async_copy(source, target, load_sem.at[m, len(group)]))
        loads.append(group)
    norm_loads = [
        pltpu.make_async_copy(norms[i], norm_mem.at[i], load_sem.at[3, i]) for i in range(2)
    ]
    for group in loads:
        for copy in group:
            copy.start()
    for copy in norm_loads:
        copy.start()

    barrier = pltpu.get_barrier_semaphore()
    for step in range(1, n):
        pl.semaphore_signal(
            barrier, inc=1, device_id={"shard": lax.rem(me + step, n)}, device_id_type=MESH
        )
    for step in range(1, width):
        pl.semaphore_signal(
            barrier, inc=1, device_id={"width": lax.rem(line + step, width)}, device_id_type=MESH
        )

    tile = piece

    def merge(m):
        for copy in loads[m]:
            copy.wait()
        low_mem[m] = low_turned[m].T

        def body(t, largest):
            at = pl.ds(pl.multiple_of(t * tile, tile), tile)
            value = w_mem[m, at, :].astype(jnp.float32) + mix_rate * jnp.dot(
                low_mem[m, at, :], high_mem[m], preferred_element_type=jnp.float32
            )
            latest[m, at, :] = value
            return jnp.maximum(largest, jnp.max(jnp.abs(value), axis=0, keepdims=True))

        largest = lax.fori_loop(0, rows // tile, body, jnp.zeros((1, w_mem.shape[2]), jnp.float32))
        maxima[m, me] = largest

    def share(m):
        for step in range(1, n):
            pltpu.make_async_remote_copy(
                src_ref=maxima.at[m, me],
                dst_ref=maxima.at[m, me],
                send_sem=max_send.at[m],
                recv_sem=max_recv.at[m],
                device_id={"shard": lax.rem(me + step, n)},
                device_id_type=MESH,
            ).start()

    def settle(m):
        others = maxima.at[m, pl.ds(0, n - 1)]
        pltpu.make_async_copy(others, others, max_recv.at[m]).wait()
        factor = jnp.max(maxima[m], axis=0)
        factors[m][...] = factor
        scale[m] = 1.0 / factor

    def rows_of(letter, k):
        return ((letter * count) + k % count) * piece

    def finish(k):
        m = k // count
        for letter in range(2):
            at = pl.ds(rows_of(letter, k), piece)
            ready[m, me, at, :] = (latest[m, at, :] * scale[m]).astype(jnp.bfloat16)

    def view(k, letter, owner):
        return outs[k // count].at[owner, pl.ds(rows_of(letter, k), piece)]

    def ring_copy(k, side, letter, hop):
        sign = 1 - 2 * side
        owner = shard_at(-sign * hop)
        where = view(k, letter, owner)
        return pltpu.make_async_remote_copy(
            src_ref=where,
            dst_ref=where,
            send_sem=send_sem.at[k // count],
            recv_sem=ring_sem.at[k, side, letter, hop],
            device_id={"shard": shard_at(sign)},
            device_id_type=MESH,
        )

    def ring_arrival(k, side, letter, hop):
        sign = 1 - 2 * side
        owner = shard_at(-sign * (hop + 1))
        where = view(k, letter, owner)
        pltpu.make_async_copy(where, where, ring_sem.at[k, side, letter, hop]).wait()
        return owner

    def pair_copy(k, letter, owner):
        where = view(k, letter, owner)
        pltpu.make_async_remote_copy(
            src_ref=where,
            dst_ref=where,
            send_sem=send_sem.at[k // count],
            recv_sem=pair_sem.at[k // count],
            device_id={"shard": sibling},
            device_id_type=MESH,
        ).start()

    def hops(side, letter):
        return half if side == letter else half - 1

    merge(0)
    pl.semaphore_wait(barrier, n - 1 + width - 1)
    share(0)
    for copy in norm_loads:
        copy.wait()
    gains[me, line] = norm_mem[0] + norm_mem[1]
    for step in range(1, width):
        pltpu.make_async_remote_copy(
            src_ref=gains.at[me, line],
            dst_ref=gains.at[me, line],
            send_sem=norm_send.at[0],
            recv_sem=norm_recv.at[0],
            device_id={"width": lax.rem(line + step, width)},
            device_id_type=MESH,
        ).start()
    merge(1)
    share(1)
    settle(0)
    finish(0)

    for j in range(steps + half + 1):
        if j < steps:
            for side in range(2):
                if hops(side, side) > 0:
                    ring_copy(j, side, side, 0).start()
        for hop in range(half):
            k = j - 1 - hop
            if 0 <= k < steps and hop + 1 < half:
                for side in range(2):
                    owner = ring_arrival(k, side, side, hop)
                    ring_copy(k, side, side, hop + 1).start()
                    pair_copy(k, side, owner)
        if j < steps:
            for side in range(2):
                if hops(side, 1 - side) > 0:
                    ring_copy(j, side, 1 - side, 0).start()
        for hop in range(half - 1):
            k = j - 1 - hop
            if 0 <= k < steps and hop + 1 < half - 1:
                for side in range(2):
                    owner = ring_arrival(k, side, 1 - side, hop)
                    ring_copy(k, side, 1 - side, hop + 1).start()
                    pair_copy(k, 1 - side, owner)
        if j < steps:
            for letter in range(2):
                pair_copy(j, letter, me)
        if j == 0:
            merge(2)
            share(2)
            ours = gains.at[me, pl.ds(0, width - 1)]
            if width > 1:
                pltpu.make_async_copy(ours, ours, norm_recv.at[0]).wait()
            for step in range(1, n):
                pltpu.make_async_remote_copy(
                    src_ref=gains.at[me],
                    dst_ref=gains.at[me],
                    send_sem=norm_send.at[1],
                    recv_sem=norm_recv.at[1],
                    device_id={"shard": lax.rem(me + step, n)},
                    device_id_type=MESH,
                ).start()
        if j + 1 < steps:
            if (j + 1) % count == 0:
                settle((j + 1) // count)
            finish(j + 1)
        for side in range(2):
            for letter in (side, 1 - side):
                hop = hops(side, letter) - 1
                k = j - 2 - hop
                if hop >= 0 and 0 <= k < steps:
                    owner = ring_arrival(k, side, letter, hop)
                    pair_copy(k, letter, owner)

    for m in range(3):
        theirs = outs[m].at[pl.ds(0, chips)]
        pltpu.make_async_copy(theirs, theirs, pair_sem.at[m]).wait()
        sent = outs[m].at[pl.ds(0, n - 1)]
        pltpu.make_async_copy(sent, sent, send_sem.at[m]).wait()
        others = maxima.at[m, pl.ds(0, n - 1)]
        pltpu.make_async_copy(others, others, max_send.at[m]).wait()
    ours = gains.at[me, pl.ds(0, width - 1)]
    pltpu.make_async_copy(ours, ours, norm_send.at[0]).wait()
    block = gains.at[pl.ds(0, n - 1)]
    pltpu.make_async_copy(block, block, norm_recv.at[1]).wait()
    pltpu.make_async_copy(block, block, norm_send.at[1]).wait()


def place_kernel(*refs):
    source, targets, sem = refs[0], refs[1:4], refs[4]
    copies = []
    for m in range(3):
        for i in range(source.shape[1]):
            copies.append(
                pltpu.make_async_copy(source.at[m, i], targets[m].at[i], sem.at[m, i])
            )
    for copy in copies:
        copy.start()
    for copy in copies:
        copy.wait()


def body(n, width, w_query, low_query, high_query, w_key, low_key, high_key, w_value, low_value, high_value, norm_train, norm_step):
    rows, columns = w_query.shape
    rank = low_query.shape[1]
    length = norm_train.shape[0]
    half = n // 4
    steps = 3 * chunks_of(rows)
    results = pl.pallas_call(
        functools.partial(gather_kernel, n, width),
        name="merge_gather",
        out_shape=[pltpu.VMEM((3, n, rows, columns), jnp.bfloat16)]
        + [jax.ShapeDtypeStruct((1, columns), jnp.float32)] * 3
        + [jax.ShapeDtypeStruct((n, width, 1, length), jnp.float32)],
        in_specs=[ANY] * 11,
        out_specs=[pl.BlockSpec(memory_space=pltpu.VMEM)] * 5,
        scratch_shapes=[
            pltpu.VMEM((3, rows, columns), jnp.bfloat16),
            pltpu.VMEM((3, rows, rank), jnp.bfloat16),
            pltpu.VMEM((3, rank, columns), jnp.bfloat16),
            pltpu.VMEM((2, 1, length), jnp.float32),
            pltpu.VMEM((3, rows, columns), jnp.float32),
            pltpu.VMEM((3, 1, columns), jnp.float32),
            pltpu.VMEM((3, n, 1, columns), jnp.float32),
            pltpu.SemaphoreType.DMA((4, 3)),
            pltpu.SemaphoreType.DMA((3,)),
            pltpu.SemaphoreType.DMA((3,)),
            pltpu.SemaphoreType.DMA((3,)),
            pltpu.SemaphoreType.DMA((2,)),
            pltpu.SemaphoreType.DMA((2,)),
            pltpu.SemaphoreType.DMA((steps, 2, 2, half)),
            pltpu.SemaphoreType.DMA((3,)),
            pltpu.VMEM((3, rank, rows), jnp.bfloat16),
        ],
        compiler_params=pltpu.CompilerParams(
            collective_id=0, has_side_effects=True, vmem_limit_bytes=20 * 2**20
        ),
    )(
        w_query, w_key, w_value,
        low_query.T, low_key.T, low_value.T,
        high_query, high_key, high_value,
        norm_train.reshape(1, length), norm_step.reshape(1, length),
    )
    readies = pl.pallas_call(
        place_kernel,
        name="place",
        out_shape=[jax.ShapeDtypeStruct((n, rows, columns), jnp.bfloat16)] * 3,
        in_specs=[ANY],
        out_specs=[ANY] * 3,
        scratch_shapes=[pltpu.SemaphoreType.DMA((3, n))],
        compiler_params=pltpu.CompilerParams(vmem_limit_bytes=2**20),
    )(pltpu.with_memory_space_constraint(results[0], pltpu.VMEM))
    return (
        *(ready.reshape(n * rows, columns) for ready in readies),
        *(factor.reshape(columns) for factor in results[1:4]),
        results[4].astype(jnp.bfloat16).reshape(n * width * length),
    )


def solution(mesh):
    n, width = mesh.shape["shard"], mesh.shape["width"]
    return jax.shard_map(
        functools.partial(body, n, width),
        mesh=mesh,
        in_specs=(
            P("shard", "width"),
            P("shard", None),
            P(None, "width"),
            P("shard", "width"),
            P("shard", None),
            P(None, "width"),
            P("shard", "width"),
            P("shard", None),
            P(None, "width"),
            P(("shard", "width")),
            P(("shard", "width")),
        ),
        out_specs=(
            P(None, "width"),
            P(None, "width"),
            P(None, "width"),
            P("width"),
            P("width"),
            P("width"),
            P(),
        ),
        check_vma=False,
    )
```

time: 305 us -> 189 us (0.62)
  Pallas kernels: 0 us -> 186 us
  waiting for transfers between devices: 181 us -> 0 us
  blocking collectives: 66.4 us -> 0 us
  local copies, waits for them, and re-layouts: 27.9 us -> 0.71 us
  between operations: 13.9 us -> 0.7 us
  matrix products: 6.87 us -> 0 us
  other arithmetic: 8.07 us -> 1.95 us
    pallas_call x0 -> x2, Pallas kernels: none -> 186 us  [the longest x1 173 us: body(): pl.pallas_call(functools.partial(gather_kernel, n, width), name='merge_ga...]
    all_gather x3 -> x0, waiting for transfers between devices: 181 us -> none  [the longest x1 76.7 us: body(): lax.all_gather(narrow_query, 'shard', axis=0, tiled=True)]
    unnamed x1 -> x0, blocking collectives: 40.9 us -> none
    unnamed x41 -> x8, local copies, waits for them, and re-layouts: 27.9 us -> 0.02 us
    pmax x1 -> x0, blocking collectives: 25.5 us -> none  [body(): lax.pmax((jnp.max(jnp.abs(latest_query), axis=0), jnp.max(jnp.abs(latest_...]
    convert_element_type x4 -> x1, other arithmetic: 8.07 us -> 0.09 us  [body(): results[4].astype(jnp.bfloat16).reshape(n * width * length)]
    dot_general x3 -> x0, matrix products: 6.87 us -> none  [the longest x1 2.33 us: body(): jnp.dot(low_value, high_value, preferred_element_type=jnp.float32)]
  transfers between devices with their start and end apart: 3 -> 0, of which waited for: 3 -> 0; matrix products, arithmetic and copies ran while one was open for 2% -> 0% of each run, Pallas kernels for 0% -> 0%
where the time goes in v1:
time: 189 us
  Pallas kernels  186 us (98%)
  other arithmetic  1.95 us (1%)
    pallas_call x1, Pallas kernels, body(): pl.pallas_call(functools.partial(gather_kernel, n, width), name='merge_ga...  173 us
    pallas_call x1, Pallas kernels, body(): pl.pallas_call(place_kernel, name='place', out_shape=[jax.ShapeDtypeStruc...  12.9 us

profile of v1, /device:TPU:0, one launch (start us, length us, event | category | flops | bytes accessed | tf_op | source)
XLA Modules:
  0.0 189.2 jit_solution(15463571457362701447)
XLA Ops:
  0.6 173.0 %merge_gather.1 = (bf16[3,8,640,1280]{3,2,1,0:T(8,128)(2,1)S(1)}, f32[1,1280]{1,0:T(1,128)}, f32[1,1280]{1,0:T(1,128)}, f32[1,1280]{1,0:T(1,128)}, f32[8,4,1,160]{3,2,1,0:T(1,128)}) custom-call(bf16[640,1280]{1,0:T(8,128)(2,1)} %refs_0_.1, bf16[640,1280]{1,0:T(8,128)(2,1)} %refs_1_.1, bf16[640,1280]{1,0:T(8,128)(2,1)} %refs_2_.1, bf16[32,640]{1,0:T(8,128)(2,1)} %bitcast.8, ...), custom_call_target="tpu_custom_call" | custom-call | tf_op jit(solution)/shard_map/merge_gather/pallas_call | solution.py:268
  173.7 0.0 copy-start.3
  173.7 0.0 copy-start.2
  173.7 0.0 copy-start.1
  173.7 0.0 copy-start
  173.7 12.9 %place.1 = (bf16[8,640,1280]{2,1,0:T(8,128)(2,1)}, bf16[8,640,1280]{2,1,0:T(8,128)(2,1)}, bf16[8,640,1280]{2,1,0:T(8,128)(2,1)}) custom-call(bf16[3,8,640,1280]{3,2,1,0:T(8,128)(2,1)S(1)} %get-tuple-element.15.refs_0_), custom_call_target="tpu_custom_call" | custom-call | tf_op jit(solution)/shard_map/place/pallas_call | solution.py:303
  186.6 0.0 copy-done.3
  186.6 0.6 reduce
  187.2 0.0 copy-done.2
  187.2 0.6 reduce.1
  187.8 0.0 copy-done.1
  187.8 0.6 reduce.2
  188.5 0.0 copy-done
  188.5 0.1 convert_reduce_fusion
  188.6 0.7 reshape.49
Async XLA Ops:
  173.7 12.9 %copy-start.3 = (f32[1,1280]{1,0:T(1,128)S(1)}, f32[1,1280]{1,0:T(1,128)}, u32[]{:S(2)}) copy-start(f32[1,1280]{1,0:T(1,128)} %get-tuple-element.19) | copy-start | bytes 15364
  173.7 13.5 %copy-start.2 = (f32[1,1280]{1,0:T(1,128)S(1)}, f32[1,1280]{1,0:T(1,128)}, u32[]{:S(2)}) copy-start(f32[1,1280]{1,0:T(1,128)} %get-tuple-element.20) | copy-start | bytes 15364
  173.7 14.1 %copy-start.1 = (f32[1,1280]{1,0:T(1,128)S(1)}, f32[1,1280]{1,0:T(1,128)}, u32[]{:S(2)}) copy-start(f32[1,1280]{1,0:T(1,128)} %get-tuple-element.21) | copy-start | bytes 15364
  173.7 14.7 %copy-start = (f32[8,4,1,160]{3,2,1,0:T(1,128)S(1)}, f32[8,4,1,160]{3,2,1,0:T(1,128)}, u32[]{:S(2)}) copy-start(f32[8,4,1,160]{3,2,1,0:T(1,128)} %get-tuple-element.22) | copy-start | bytes 61444

commit v2 on v1

--- a/solution.py
+++ b/solution.py
@@ -89,10 +89,11 @@
                 low_mem[m, at, :], high_mem[m], preferred_element_type=jnp.float32
             )
             latest[m, at, :] = value
-            return jnp.maximum(largest, jnp.max(jnp.abs(value), axis=0, keepdims=True))
-
-        largest = lax.fori_loop(0, rows // tile, body, jnp.zeros((1, w_mem.shape[2]), jnp.float32))
-        maxima[m, me] = largest
+            sizes = jnp.abs(value).reshape(tile // 8, 8, value.shape[1])
+            return jnp.maximum(largest, jnp.max(sizes, axis=0))
+
+        largest = lax.fori_loop(0, rows // tile, body, jnp.zeros((8, w_mem.shape[2]), jnp.float32))
+        maxima[m, me] = jnp.max(largest, axis=0, keepdims=True)
 
     def share(m):
         for step in range(1, n):
@@ -161,20 +162,6 @@
     merge(0)
     pl.semaphore_wait(barrier, n - 1 + width - 1)
     share(0)
-    for copy in norm_loads:
-        copy.wait()
-    gains[me, line] = norm_mem[0] + norm_mem[1]
-    for step in range(1, width):
-        pltpu.make_async_remote_copy(
-            src_ref=gains.at[me, line],
-            dst_ref=gains.at[me, line],
-            send_sem=norm_send.at[0],
-            recv_sem=norm_recv.at[0],
-            device_id={"width": lax.rem(line + step, width)},
-            device_id_type=MESH,
-        ).start()
-    merge(1)
-    share(1)
     settle(0)
     finish(0)
 
@@ -205,6 +192,21 @@
             for letter in range(2):
                 pair_copy(j, letter, me)
         if j == 0:
+            merge(1)
+            share(1)
+            for copy in norm_loads:
+                copy.wait()
+            gains[me, line] = norm_mem[0] + norm_mem[1]
+            for step in range(1, width):
+                pltpu.make_async_remote_copy(
+                    src_ref=gains.at[me, line],
+                    dst_ref=gains.at[me, line],
+                    send_sem=norm_send.at[0],
+                    recv_sem=norm_recv.at[0],
+                    device_id={"width": lax.rem(line + step, width)},
+                    device_id_type=MESH,
+                ).start()
+        if j == 1:
             merge(2)
             share(2)
             ours = gains.at[me, pl.ds(0, width - 1)]
@@ -246,7 +248,14 @@
 
 
 def place_kernel(*refs):
-    source, targets, sem = refs[0], refs[1:4], refs[4]
+    source, small = refs[0], refs[1:5]
+    targets, scales, serve, sem = refs[5:8], refs[8:11], refs[11], refs[12]
+    factors, gains, small_sem = refs[13:16], refs[16], refs[17]
+    loads = [
+        pltpu.make_async_copy(small[i], refs[13 + i], small_sem.at[i]) for i in range(4)
+    ]
+    for copy in loads:
+        copy.start()
     copies = []
     for m in range(3):
         for i in range(source.shape[1]):
@@ -255,6 +264,13 @@
             )
     for copy in copies:
         copy.start()
+    for copy in loads:
+        copy.wait()
+    for m in range(3):
+        scales[m][...] = factors[m][...].reshape(scales[m].shape)
+    blocks = [gains[i, k] for i in range(gains.shape[0]) for k in range(gains.shape[1])]
+    line = jnp.concatenate(blocks, axis=1)
+    serve[...] = line.reshape(serve.shape).astype(jnp.bfloat16)
     for copy in copies:
         copy.wait()
 
@@ -300,19 +316,25 @@
         high_query, high_key, high_value,
         norm_train.reshape(1, length), norm_step.reshape(1, length),
     )
-    readies = pl.pallas_call(
+    placed = pl.pallas_call(
         place_kernel,
         name="place",
-        out_shape=[jax.ShapeDtypeStruct((n, rows, columns), jnp.bfloat16)] * 3,
-        in_specs=[ANY],
-        out_specs=[ANY] * 3,
-        scratch_shapes=[pltpu.SemaphoreType.DMA((3, n))],
+        out_shape=[jax.ShapeDtypeStruct((n, rows, columns), jnp.bfloat16)] * 3
+        + [jax.ShapeDtypeStruct((columns,), jnp.float32)] * 3
+        + [jax.ShapeDtypeStruct((n * width * length,), jnp.bfloat16)],
+        in_specs=[ANY] + [pl.BlockSpec(memory_space=pltpu.HBM)] * 4,
+        out_specs=[ANY] * 3 + [pl.BlockSpec(memory_space=pltpu.VMEM)] * 4,
+        scratch_shapes=[
+            pltpu.SemaphoreType.DMA((3, n)),
+            *[pltpu.VMEM((1, columns), jnp.float32)] * 3,
+            pltpu.VMEM((n, width, 1, length), jnp.float32),
+            pltpu.SemaphoreType.DMA((4,)),
+        ],
         compiler_params=pltpu.CompilerParams(vmem_limit_bytes=2**20),
-    )(pltpu.with_memory_space_constraint(results[0], pltpu.VMEM))
+    )(pltpu.with_memory_space_constraint(results[0], pltpu.VMEM), *(pltpu.with_memory_space_constraint(small, pltpu.HBM) for small in results[1:]))
     return (
-        *(ready.reshape(n * rows, columns) for ready in readies),
-        *(factor.reshape(columns) for factor in results[1:4]),
-        results[4].astype(jnp.bfloat16).reshape(n * width * length),
+        *(ready.reshape(n * rows, columns) for ready in placed[0:3]),
+        *placed[3:],
     )
 
 

time: 189 us -> 188 us (level)
  other arithmetic: 1.95 us -> 0 us
where the time goes in v2:
time: 188 us
  Pallas kernels  187 us (99%)
    pallas_call x1, Pallas kernels, body(): pl.pallas_call(functools.partial(gather_kernel, n, width), name='merge_ga...  173 us
    pallas_call x1, Pallas kernels, body(): pl.pallas_call(place_kernel, name='place', out_shape=[jax.ShapeDtypeStruc...  13.5 us

profile of v2, /device:TPU:0, one launch (start us, length us, event | category | flops | bytes accessed | tf_op | source)
XLA Modules:
  0.0 187.5 jit_solution(6858210990160072999)
XLA Ops:
  0.6 173.4 %merge_gather.1 = (bf16[3,8,640,1280]{3,2,1,0:T(8,128)(2,1)S(1)}, f32[1,1280]{1,0:T(1,128)}, f32[1,1280]{1,0:T(1,128)}, f32[1,1280]{1,0:T(1,128)}, f32[8,4,1,160]{3,2,1,0:T(1,128)}) custom-call(bf16[640,1280]{1,0:T(8,128)(2,1)} %refs_0_.1, bf16[640,1280]{1,0:T(8,128)(2,1)} %refs_1_.1, bf16[640,1280]{1,0:T(8,128)(2,1)} %refs_2_.1, bf16[32,640]{1,0:T(8,128)(2,1)} %bitcast.8, ...), custom_call_target="tpu_custom_call" | custom-call | tf_op jit(solution)/shard_map/merge_gather/pallas_call | solution.py:284
  174.0 13.5 %place.1 = (bf16[8,640,1280]{2,1,0:T(8,128)(2,1)}, bf16[8,640,1280]{2,1,0:T(8,128)(2,1)}, bf16[8,640,1280]{2,1,0:T(8,128)(2,1)}, f32[1280]{0:T(1024)}, f32[1280]...) custom-call(bf16[3,8,640,1280]{3,2,1,0:T(8,128)(2,1)S(1)} %get-tuple-element.19.refs_0_, ...), custom_call_target="tpu_custom_call" | custom-call | tf_op jit(solution)/shard_map/place/pallas_call | solution.py:319

commit v3 on v2

--- a/solution.py
+++ b/solution.py
@@ -21,10 +21,10 @@
 
 def gather_kernel(n, width, *refs):
     weights, lows, highs, norms = refs[0:3], refs[3:6], refs[6:9], refs[9:11]
-    ready, factors, gains = refs[11], refs[12:15], refs[15]
+    ready, small_outs = refs[11], refs[12:16]
     w_mem, low_mem, high_mem, norm_mem, latest, scale, maxima = refs[16:23]
     load_sem, send_sem, max_send, max_recv, norm_send, norm_recv = refs[23:29]
-    ring_sem, pair_sem, low_turned = refs[29:32]
+    ring_sem, pair_sem, low_turned, held, gains, out_sem = refs[29:35]
     outs = [ready.at[m] for m in range(3)]
 
     rows = w_mem.shape[1]
@@ -110,7 +110,7 @@
         others = maxima.at[m, pl.ds(0, n - 1)]
         pltpu.make_async_copy(others, others, max_recv.at[m]).wait()
         factor = jnp.max(maxima[m], axis=0)
-        factors[m][...] = factor
+        held[m] = factor
         scale[m] = 1.0 / factor
 
     def rows_of(letter, k):
@@ -159,6 +159,9 @@
     def hops(side, letter):
         return half if side == letter else half - 1
 
+    small_writes = [
+        pltpu.make_async_copy(held.at[m], small_outs[m], out_sem.at[m]) for m in range(3)
+    ] + [pltpu.make_async_copy(gains, small_outs[3], out_sem.at[3])]
     merge(0)
     pl.semaphore_wait(barrier, n - 1 + width - 1)
     share(0)
@@ -221,6 +224,11 @@
                     device_id={"shard": lax.rem(me + step, n)},
                     device_id_type=MESH,
                 ).start()
+        if j == steps - 1:
+            block = gains.at[pl.ds(0, n - 1)]
+            pltpu.make_async_copy(block, block, norm_recv.at[1]).wait()
+            for copy in small_writes:
+                copy.start()
         if j + 1 < steps:
             if (j + 1) % count == 0:
                 settle((j + 1) // count)
@@ -243,14 +251,19 @@
     ours = gains.at[me, pl.ds(0, width - 1)]
     pltpu.make_async_copy(ours, ours, norm_send.at[0]).wait()
     block = gains.at[pl.ds(0, n - 1)]
-    pltpu.make_async_copy(block, block, norm_recv.at[1]).wait()
     pltpu.make_async_copy(block, block, norm_send.at[1]).wait()
+    for copy in small_writes:
+        copy.wait()
 
 
 def place_kernel(*refs):
     source, small = refs[0], refs[1:5]
-    targets, scales, serve, sem = refs[5:8], refs[8:11], refs[11], refs[12]
+    targets, finals, sem = refs[5:8], refs[8:12], refs[12]
     factors, gains, small_sem = refs[13:16], refs[16], refs[17]
+    scales, serve = refs[18:21], refs[21]
+    writes = [
+        pltpu.make_async_copy(refs[18 + i], finals[i], small_sem.at[4 + i]) for i in range(4)
+    ]
     loads = [
         pltpu.make_async_copy(small[i], refs[13 + i], small_sem.at[i]) for i in range(4)
     ]
@@ -271,7 +284,10 @@
     blocks = [gains[i, k] for i in range(gains.shape[0]) for k in range(gains.shape[1])]
     line = jnp.concatenate(blocks, axis=1)
     serve[...] = line.reshape(serve.shape).astype(jnp.bfloat16)
-    for copy in copies:
+    copies[0].wait()
+    for copy in writes:
+        copy.start()
+    for copy in copies[1:] + writes:
         copy.wait()
 
 
@@ -288,7 +304,8 @@
         + [jax.ShapeDtypeStruct((1, columns), jnp.float32)] * 3
         + [jax.ShapeDtypeStruct((n, width, 1, length), jnp.float32)],
         in_specs=[ANY] * 11,
-        out_specs=[pl.BlockSpec(memory_space=pltpu.VMEM)] * 5,
+        out_specs=[pl.BlockSpec(memory_space=pltpu.VMEM)]
+        + [pl.BlockSpec(memory_space=pltpu.HBM)] * 4,
         scratch_shapes=[
             pltpu.VMEM((3, rows, columns), jnp.bfloat16),
             pltpu.VMEM((3, rows, rank), jnp.bfloat16),
@@ -306,6 +323,9 @@
             pltpu.SemaphoreType.DMA((steps, 2, 2, half)),
             pltpu.SemaphoreType.DMA((3,)),
             pltpu.VMEM((3, rank, rows), jnp.bfloat16),
+            pltpu.VMEM((3, 1, columns), jnp.float32),
+            pltpu.VMEM((n, width, 1, length), jnp.float32),
+            pltpu.SemaphoreType.DMA((4,)),
         ],
         compiler_params=pltpu.CompilerParams(
             collective_id=0, has_side_effects=True, vmem_limit_bytes=20 * 2**20
@@ -323,12 +343,14 @@
         + [jax.ShapeDtypeStruct((columns,), jnp.float32)] * 3
         + [jax.ShapeDtypeStruct((n * width * length,), jnp.bfloat16)],
         in_specs=[ANY] + [pl.BlockSpec(memory_space=pltpu.HBM)] * 4,
-        out_specs=[ANY] * 3 + [pl.BlockSpec(memory_space=pltpu.VMEM)] * 4,
+        out_specs=[ANY] * 3 + [pl.BlockSpec(memory_space=pltpu.HBM)] * 4,
         scratch_shapes=[
             pltpu.SemaphoreType.DMA((3, n)),
             *[pltpu.VMEM((1, columns), jnp.float32)] * 3,
             pltpu.VMEM((n, width, 1, length), jnp.float32),
-            pltpu.SemaphoreType.DMA((4,)),
+            pltpu.SemaphoreType.DMA((8,)),
+            *[pltpu.VMEM((columns,), jnp.float32)] * 3,
+            pltpu.VMEM((n * width * length,), jnp.bfloat16),
         ],
         compiler_params=pltpu.CompilerParams(vmem_limit_bytes=2**20),
     )(pltpu.with_memory_space_constraint(results[0], pltpu.VMEM), *(pltpu.with_memory_space_constraint(small, pltpu.HBM) for small in results[1:]))

time: 188 us -> 187 us (level)
  no operation moved by 1% of the time
where the time goes in v3:
time: 187 us; the launch traced here: 186 us
  Pallas kernels  186 us (99%)
    pallas_call x1, Pallas kernels, body(): pl.pallas_call(functools.partial(gather_kernel, n, width), name='merge_ga...  173 us
    pallas_call x1, Pallas kernels, body(): pl.pallas_call(place_kernel, name='place', out_shape=[jax.ShapeDtypeStruc...  12.9 us

profile of v3, /device:TPU:0, one launch (start us, length us, event | category | flops | bytes accessed | tf_op | source)
XLA Modules:
  0.0 186.4 jit_solution(6383398306800230098)
XLA Ops:
  0.6 172.8 %merge_gather.1 = (bf16[3,8,640,1280]{3,2,1,0:T(8,128)(2,1)S(1)}, f32[1,1280]{1,0:T(1,128)}, f32[1,1280]{1,0:T(1,128)}, f32[1,1280]{1,0:T(1,128)}, f32[8,4,1,160]{3,2,1,0:T(1,128)}) custom-call(bf16[640,1280]{1,0:T(8,128)(2,1)} %refs_0_.1, bf16[640,1280]{1,0:T(8,128)(2,1)} %refs_1_.1, bf16[640,1280]{1,0:T(8,128)(2,1)} %refs_2_.1, bf16[32,640]{1,0:T(8,128)(2,1)} %bitcast.8, ...), custom_call_target="tpu_custom_call" | custom-call | tf_op jit(solution)/shard_map/merge_gather/pallas_call | solution.py:300
  173.4 12.9 %place.1 = (bf16[8,640,1280]{2,1,0:T(8,128)(2,1)}, bf16[8,640,1280]{2,1,0:T(8,128)(2,1)}, bf16[8,640,1280]{2,1,0:T(8,128)(2,1)}, f32[1280]{0:T(1024)}, f32[1280]...) custom-call(bf16[3,8,640,1280]{3,2,1,0:T(8,128)(2,1)S(1)} %get-tuple-element.19.refs_0_, ...), custom_call_target="tpu_custom_call" | custom-call | tf_op jit(solution)/shard_map/place/pallas_call | solution.py:339
